TPU v7x, 32 devices: a whole 2x2x4 slice. The times are simulated.
32 devices in a mesh: frame: 4 (over x, core), seq: 8 (over z, y).
Axes of the slice: x: 2, y: 2, z: 4, core: 2. Of those that a mesh axis runs over, the one named last changes fastest.
Arguments:
- vit_states: bfloat16 [64, 256, 1280], P(('frame', 'seq')), may hold values from -6 to 6
- frame_slot: int32 [32], replicated, may hold values from 0 to 63, as said below
- patch_count: int32 [32], replicated, may hold values from 208 to 256, as said below
- vis_start: int32 [32], replicated, may hold values from 0 to 4095, as said below
- text_embed: bfloat16 [128, 32, 4096], P(None, ('frame', 'seq')), may hold values from -6 to 6
- vit_ln_gain: float32 [1280], replicated, may hold values from 0.25 to 1.75
- vit_ln_bias: float32 [1280], replicated, may hold values from -1.5 to 1.5
- vit_qkv_w: bfloat16 [1280, 3840], P('seq'), may hold values from -0.15625 to 0.15625
- vit_qkv_b: float32 [3840], replicated, may hold values from -1.5 to 1.5
- vit_out_w: bfloat16 [1280, 1280], P('seq'), may hold values from -0.15625 to 0.15625
- vit_out_b: float32 [1280], replicated, may hold values from -1.5 to 1.5
- proj_w: bfloat16 [1280, 4096], replicated, may hold values from -0.15625 to 0.15625
- proj_b: float32 [4096], replicated, may hold values from -1.5 to 1.5
- attn_gain: float32 [4096], replicated, may hold values from 0.25 to 1.75
- wq: bfloat16 [4096, 2048], P(None, 'frame'), may hold values from -0.09375 to 0.09375
- wk: bfloat16 [4096, 1024], P(None, 'frame'), may hold values from -0.09375 to 0.09375
- wv: bfloat16 [4096, 1024], P(None, 'frame'), may hold values from -0.09375 to 0.09375
- wo: bfloat16 [2048, 4096], P('frame'), may hold values from -0.125 to 0.125
Outputs:
- mixed: bfloat16 [128, 32, 4096], P(None, ('frame', 'seq'))
Inputs may be any that keep to these rules, and one draw needn't show every extreme that they name: Frame t sits in slot frame_slot[t]; slot k of the device with index d (axes frame then seq) is d * 2 + k; no slot holds two frames. The two devices with frame indices 2i and 2i+1 and the same seq index hold exactly two frames between them; some device holds 2 frames. `patch_count`: A multiple of 4; some frame has 256 patches. Frame t's patch_count[t] / 4 visual positions start at vis_start[t] and lie within positions t * 128 to (t + 1) * 128 - 1.
All inputs are finite; a program needn't handle non-finite values.
Results may differ from a plain program's by a relative error of at most 0.015.
Values may be sent and summed in bfloat16 or wider, within the bound.
A program may use at most 128 MiB of HBM per device.

v0:
```python
import math
import jax
import jax.numpy as jnp
from jax import lax
from jax.sharding import PartitionSpec as P

VHEADS = 16
HEAD_WIDTH = 128
rope_theta = 500000.0
vit_epsilon = 1e-06
norm_epsilon = 1e-05
masked_score = -1e30


def partner_2(value, axis, stride):
    mask = 2**stride
    pairs = [(source, source ^ mask) for source in range(lax.axis_size(axis))]
    return lax.ppermute(value, axis, pairs)


def apply_rotary(values, rotary_angles):
    half_width = values.shape[-1] // 2
    first_half = values[..., :half_width]
    second_half = values[..., half_width:]
    cosine = jnp.cos(rotary_angles)
    sine_part = jnp.sin(rotary_angles)
    return jnp.concatenate(
        [
            first_half * cosine - second_half * sine_part,
            second_half * cosine + first_half * sine_part,
        ],
        axis=-1,
    )


def rope_angles(positions, head_size):
    exponents = jnp.arange(0, head_size, 2).astype(jnp.float32) / head_size
    inverse = jnp.power(jnp.float32(rope_theta), -exponents)
    return positions.astype(jnp.float32)[:, None] * inverse[None, :]


def add_columns(left, shard_piece):
    return jnp.dot(left, shard_piece, preferred_element_type=jnp.float32)


def per_device(
    vit_states,
    frame_slot,
    patch_count,
    vis_start,
    text_embed,
    vit_ln_gain,
    vit_ln_bias,
    vit_qkv_w,
    vit_qkv_b,
    vit_out_w,
    vit_out_b,
    proj_w,
    proj_b,
    attn_gain,
    wq,
    wk,
    wv,
    wo,
):
    frames_n = lax.axis_size("frame")
    seqs_n = lax.axis_size("seq")
    devices_n = frames_n * seqs_n
    my_frame = lax.axis_index("frame")
    my_seq = lax.axis_index("seq")
    my_device = my_frame * seqs_n + my_seq
    slots_held = vit_states.shape[0]
    frame_max = vit_states.shape[1]
    width_vit = vit_states.shape[2]
    vis_max = frame_max // 4
    own_rows = text_embed.shape[0]
    laps = (vis_max + devices_n - 1) // devices_n
    frame_ids = jnp.arange(frame_slot.shape[0])
    holder = frame_slot // slots_held
    holder_frame = holder // seqs_n
    pair_low = (holder_frame - holder_frame % 2) * seqs_n + holder % seqs_n
    pair_order = holder_frame % 2 * slots_held + frame_slot % slots_held
    same_pair = pair_low[:, None] == pair_low[None, :]
    earlier = pair_order[None, :] < pair_order[:, None]
    pair_rank = jnp.sum((same_pair & earlier).astype(jnp.int32), axis=1)
    partner = partner_2(vit_states, "frame", 0)
    low_side = my_frame % 2 == 0
    four_slots = jnp.where(
        low_side,
        jnp.concatenate([vit_states, partner], 0),
        jnp.concatenate([partner, vit_states], 0),
    )
    my_low = (my_frame - my_frame % 2) * seqs_n + my_seq
    picked = (pair_low == my_low) & (pair_rank == my_frame % 2)
    my_frame_id = jnp.sum(jnp.where(picked, frame_ids, 0))
    my_order = jnp.sum(jnp.where(picked, pair_order, 0))
    states = lax.dynamic_slice_in_dim(four_slots, my_order, 1, 0)
    slots_n = 1
    slot_frames = jnp.reshape(my_frame_id, (1,))
    slot_live = jnp.ones((1,), jnp.bool_)
    source_device = pair_low + pair_rank * seqs_n
    slot_count = jnp.where(slot_live, patch_count[slot_frames], frame_max)
    slot_start = vis_start[slot_frames]
    patch_rows = states.reshape(slots_n * frame_max, width_vit)
    rows_wide = patch_rows.astype(jnp.float32)
    average = jnp.mean(rows_wide, axis=1, keepdims=True)
    centred = rows_wide - average
    spread = jnp.mean(centred * centred, axis=1, keepdims=True)
    normed_states = (centred * lax.rsqrt(spread + vit_epsilon) * vit_ln_gain + vit_ln_bias).astype(
        jnp.bfloat16
    )
    projected_vit = add_columns(normed_states, lax.all_gather(vit_qkv_w, "seq", axis=0, tiled=True))
    projected_vit = (projected_vit + vit_qkv_b).astype(jnp.bfloat16)
    head_size = width_vit // VHEADS
    shaped = projected_vit.reshape(slots_n, frame_max, 3, VHEADS, head_size)
    scores = jnp.einsum(
        "sqhd,skhd->shqk", shaped[:, :, 0], shaped[:, :, 1], preferred_element_type=jnp.float32
    ) / math.sqrt(head_size)
    key_live = jnp.arange(frame_max)[None, :] < slot_count[:, None]
    scores = jnp.where(key_live[:, None, None, :], scores, masked_score)
    highest = jnp.max(scores, axis=-1, keepdims=True)
    weights = jnp.exp(scores - highest)
    probabilities = (weights / jnp.sum(weights, axis=-1, keepdims=True)).astype(jnp.bfloat16)
    context_vit = jnp.einsum(
        "shqk,skhd->sqhd", probabilities, shaped[:, :, 2], preferred_element_type=jnp.float32
    ).astype(jnp.bfloat16)
    context_vit = context_vit.reshape(patch_rows.shape[0], width_vit)
    attended = add_columns(context_vit, lax.all_gather(vit_out_w, "seq", axis=0, tiled=True))
    hidden = (rows_wide + attended + vit_out_b).astype(jnp.bfloat16)
    pooled = jnp.mean(
        hidden.astype(jnp.float32).reshape(slots_n, vis_max, 4, width_vit), axis=2
    ).astype(jnp.bfloat16)
    owners = jnp.arange(devices_n)
    lap_ids = jnp.arange(laps)
    distance = jnp.mod(owners[:, None] - slot_start[None, :], devices_n)
    token_ids = distance[:, :, None] + lap_ids[None, None, :] * devices_n
    sent_live = (token_ids < (slot_count // 4)[None, :, None]) & slot_live[None, :, None]
    token_clip = jnp.minimum(token_ids, vis_max - 1)
    slot_ids = jnp.arange(slots_n)[None, :, None]
    outgoing = jnp.where(
        sent_live[..., None], pooled[slot_ids, token_clip], jnp.zeros((), jnp.bfloat16)
    )
    arrived = lax.all_to_all(outgoing, ("frame", "seq"), split_axis=0, concat_axis=0, tiled=True)
    local_ids = jnp.arange(own_rows)
    positions = local_ids * devices_n + my_device
    token_frame = positions // own_rows
    within = positions - vis_start[token_frame]
    is_visual = (within >= 0) & (within < patch_count[token_frame] // 4)
    within_clip = jnp.clip(within, 0, vis_max - 1)
    flat_index = source_device[token_frame] * slots_n * laps + within_clip // devices_n
    table = arrived.reshape(devices_n * slots_n * laps, arrived.shape[-1])
    fetched = table[flat_index]
    fetched = (jnp.dot(fetched, proj_w, preferred_element_type=jnp.float32) + proj_b).astype(
        jnp.bfloat16
    )
    text_rows = text_embed.reshape(own_rows, text_embed.shape[-1])
    merged = jnp.where(is_visual[:, None], fetched, text_rows)
    merged_wide = merged.astype(jnp.float32)
    normed_tok = (
        merged_wide
        * lax.rsqrt(jnp.mean(merged_wide * merged_wide, axis=1, keepdims=True) + norm_epsilon)
        * attn_gain
    ).astype(jnp.bfloat16)
    shard_piece = lax.all_gather(normed_tok, "frame", axis=0, tiled=True)
    projected = jnp.concatenate(
        [
            jnp.dot(shard_piece, wq, preferred_element_type=jnp.float32),
            jnp.dot(shard_piece, wk, preferred_element_type=jnp.float32),
            jnp.dot(shard_piece, wv, preferred_element_type=jnp.float32),
        ],
        axis=1,
    )
    query_width = wq.shape[1]
    kv_width = wk.shape[1]
    group_rows = projected.shape[0]
    kv_heads = kv_width // HEAD_WIDTH
    query_heads = query_width // HEAD_WIDTH
    row_ids = jnp.arange(group_rows)
    group_positions = row_ids % own_rows * devices_n + row_ids // own_rows * seqs_n + my_seq
    rotary_angles = rope_angles(group_positions, HEAD_WIDTH)[:, None, :]
    query_matrix = apply_rotary(
        projected[:, :query_width].reshape(group_rows, query_heads, HEAD_WIDTH), rotary_angles
    ).astype(jnp.bfloat16)
    keys_own = apply_rotary(
        projected[:, query_width : query_width + kv_width].reshape(
            group_rows, kv_heads, HEAD_WIDTH
        ),
        rotary_angles,
    ).astype(jnp.bfloat16)
    values_own = (
        projected[:, query_width + kv_width :]
        .astype(jnp.bfloat16)
        .reshape(group_rows, kv_heads, HEAD_WIDTH)
    )
    grouped_rows = query_matrix.reshape(group_rows, kv_heads, query_heads // kv_heads, HEAD_WIDTH)
    group_size = query_heads // kv_heads
    start_state = (
        jnp.full((kv_heads, group_size, group_rows), masked_score, jnp.float32),
        jnp.zeros((kv_heads, group_size, group_rows), jnp.float32),
        jnp.zeros((kv_heads, group_size, group_rows, HEAD_WIDTH), jnp.float32),
    )
    carry = start_state
    key_piece = lax.all_gather(keys_own, "seq", axis=0, tiled=True)
    value_piece = lax.all_gather(values_own, "seq", axis=0, tiled=True)
    piece_rows = key_piece.shape[0]
    inner_rows = math.gcd(piece_rows, 1024)
    steps_n = piece_rows // inner_rows
    key_blocks = key_piece.reshape(steps_n, inner_rows, kv_heads, HEAD_WIDTH)
    value_blocks = value_piece.reshape(steps_n, inner_rows, kv_heads, HEAD_WIDTH)
    block_offsets = inner_rows * jnp.arange(steps_n)

    def visit(running, operands):
        running_max, denominator, weighted = running
        key_block, value_block, block_offset = operands
        gathered_ids = block_offset + jnp.arange(inner_rows)
        seq_of = gathered_ids // group_rows
        inner_ids = gathered_ids % group_rows
        key_positions = inner_ids % own_rows * devices_n + inner_ids // own_rows * seqs_n + seq_of
        block_scores = jnp.einsum(
            "qkgd,nkd->kgqn", grouped_rows, key_block, preferred_element_type=jnp.float32
        ) / math.sqrt(HEAD_WIDTH)
        allowed = key_positions[None, :] <= group_positions[:, None]
        block_scores = jnp.where(allowed[None, None], block_scores, masked_score)
        new_max = jnp.maximum(running_max, jnp.max(block_scores, axis=-1))
        expd = jnp.where(allowed[None, None], jnp.exp(block_scores - new_max[..., None]), 0.0)
        rescale = jnp.exp(running_max - new_max)
        denominator = denominator * rescale + jnp.sum(expd, axis=-1)
        weighted = weighted * rescale[..., None] + jnp.einsum(
            "kgqn,nkd->kgqd",
            expd.astype(jnp.bfloat16),
            value_block,
            preferred_element_type=jnp.float32,
        )
        return ((new_max, denominator, weighted), None)

    carry, unused = lax.scan(visit, carry, (key_blocks, value_blocks, block_offsets))
    final_max, denominator, weighted = carry
    context_tok = (weighted / denominator[..., None]).astype(jnp.bfloat16)
    context_tok = jnp.transpose(context_tok, (2, 0, 1, 3)).reshape(group_rows, query_width)
    summed = lax.psum_scatter(
        jnp.dot(context_tok, wo, preferred_element_type=jnp.float32).astype(jnp.bfloat16),
        "frame",
        scatter_dimension=0,
        tiled=True,
    )
    return summed.reshape(own_rows, 1, wo.shape[1])


def solution(mesh):
    return jax.shard_map(
        per_device,
        mesh=mesh,
        in_specs=(
            P(("frame", "seq"), None, None),
            P(),
            P(),
            P(),
            P(None, ("frame", "seq"), None),
            P(),
            P(),
            P("seq", None),
            P(),
            P("seq", None),
            P(),
            P(),
            P(),
            P(),
            P(None, "frame"),
            P(None, "frame"),
            P(None, "frame"),
            P("frame", None),
        ),
        out_specs=P(None, ("frame", "seq"), None),
        check_vma=False,
    )
```

profile of v0, /device:TPU:0, one launch (start us, length us, event | category | flops | bytes accessed | tf_op | source)
XLA Modules:
  0.0 512.4 jit_solution(6202785359800764585)
XLA Ops:
  26.0 1.9 convert_reduce_fusion
  28.2 126.3 %all-gather.6.cloned.1.call-done = bf16[1280,3840]{1,0:T(8,128)(2,1)} async-done(((bf16[160,3840]{1,0:T(8,128)(2,1)}), bf16[1280,3840]{1,0:T(8,128)(2,1)}) %all-gather.6.cloned.1.call-update) | async-done | bytes 9830416 | tf_op jit(solution)/shard_map/all_gather | solution.py:112
  154.5 7.9 %fusion.48 = bf16[256,3840]{1,0:T(8,128)(2,1)} fusion(bf16[1280,3840]{1,0:T(8,128)(2,1)} %all-gather.6.cloned.1.call-done, f32[3840]{0:T(1024)S(1)} %copy-done.5, bf16[1,256,1280]{2,1,0:T(8,128)(2,1)S(1)} %get-tuple-element.277, f32[1280]{0:T(1024)S(1)} %copy-done.6, f32[1280]{0:T(1024)S(1)} %copy-done.7, f32[256]{0:T(256)S(1)} %add_rsqrt_fusion, ...), kind=kOutput, calls=%fused_computation.75 | convolution fusion | flops 2520514560 | bytes 12479488 | tf_op jit(solution)/shard_map/dot_general | solution.py:43
  162.4 4.0 copy.73
  166.4 2.0 fusion.72
  168.5 1.7 fusion.102
  171.8 44.6 %all-gather.8.cloned.1.call-done = bf16[1280,1280]{1,0:T(8,128)(2,1)} async-done(((bf16[160,1280]{1,0:T(8,128)(2,1)}), bf16[1280,1280]{1,0:T(8,128)(2,1)}) %all-gather.8.cloned.1.call-update) | async-done | bytes 3276816 | tf_op jit(solution)/shard_map/all_gather | solution.py:128
  216.4 4.0 fusion.55
  226.7 3.3 all-to-all-start
  230.3 7.7 %all-to-all-done = bf16[32,1,2,1280]{3,2,1,0:T(2,128)(2,1)S(1)} async-done(((bf16[32,1,2,1280]{3,2,1,0:T(2,128)(2,1)}), bf16[32,1,2,1280]{3,2,1,0:T(2,128)(2,1)S(1)}, u32[]{:S(2)}, u32[]{:S(2)}) %all-to-all-start) | async-done | bytes 163872 | tf_op jit(solution)/shard_map/all_to_all | solution.py:143
  239.0 6.3 %multiply_reduce_fusion = (f32[128]{0:T(128)S(1)}, f32[128,4096]{1,0:T(8,128)S(1)}) fusion(bf16[128,1,4096]{2,0,1:T(8,128)(2,1)} %param.24, f32[4096]{0:T(1024)S(1)} %copy-done.3, bf16[128,1280]{1,0:T(8,128)(2,1)S(1)} %gather_fusion.4, bf16[1280,4096]{1,0:T(8,128)(2,1)} %param.31, pred[128]{0:T(512)(128)(4,1)S(1)} %compare_and_fusion.1), kind=kOutput, calls=%fused_computation.93 | convolution fusion | flops 1345322880 | bytes 13976192 | tf_op jit(solution)/shard_map/dot_general | solution.py:153
  247.5 32.0 %all-gather.10.cloned.1.call-done = bf16[512,4096]{1,0:T(8,128)(2,1)} async-done(((bf16[128,4096]{1,0:T(8,128)(2,1)}), bf16[512,4096]{1,0:T(8,128)(2,1)}) %all-gather.10.cloned.1.call-update) | async-done | bytes 4194320 | tf_op jit(solution)/shard_map/all_gather | solution.py:164
  279.5 3.5 fusion.103
  284.5 4.2 convolution_convert_fusion.1
  289.6 6.0 %fusion.104 = f32[512,512]{0,1:T(8,128)S(1)} fusion(bf16[512,4096]{1,0:T(8,128)(2,1)} %all-gather.10.cloned.1.call-done, bf16[4096,512]{1,0:T(8,128)(2,1)} %param.34), kind=kOutput, calls=%fused_computation.213 | convolution fusion | flops 2147483648 | bytes 9437184 | tf_op jit(solution)/shard_map/dot_general | solution.py:167
  296.7 37.0 %all-gather.12.cloned.1.call-done = bf16[4096,2,128]{2,0,1:T(8,128)(2,1)} async-done(((bf16[512,2,128]{2,0,1:T(8,128)(2,1)}), bf16[4096,2,128]{2,0,1:T(8,128)(2,1)}) %all-gather.12.cloned.1.call-update) | async-done | bytes 2097168 | tf_op jit(solution)/shard_map/all_gather | solution.py:203
  333.7 49.7 %all-gather.14.cloned.1.call-done = bf16[4096,2,128]{2,0,1:T(8,128)(2,1)} async-done(((bf16[512,2,128]{2,0,1:T(8,128)(2,1)}), bf16[4096,2,128]{2,0,1:T(8,128)(2,1)}) %all-gather.14.cloned.1.call-update) | async-done | bytes 2097168 | tf_op jit(solution)/shard_map/all_gather | solution.py:204
  383.3 71.8 %while.20 = (s32[]{:T(128)}, f32[2,2,512]{2,1,0:T(2,128)S(1)}, f32[2,2,512]{2,1,0:T(2,128)S(1)}, f32[2,2,512,128]{3,2,1,0:T(8,128)S(1)}, s32[4]{0:T(128)S(1)}, /...) while((s32[]{:T(128)}, f32[2,2,512]{2,1,0:T(2,128)S(1)}, ...), condition=%wide.region_12.13_spmd.clone, body=%wide.region_9.12_spmd.clone.sunk | while | flops 1102377984 | bytes 64631976 | solution.py:236
  385.0 5.9 %fusion.134 = (f32[2,2,512]{2,1,0:T(2,128)S(1)}, f32[2,1024,512,2]{2,1,3,0:T(8,128)}) fusion(pred[512,1024]{0,1:T(8,128)(4,1)S(1)} %broadcast_compare_fusion.2, bf16[512,2,2,128]{3,0,2,1:T(8,128)(2,1)S(1)} %get-tuple-element.390, bf16[4,1024,2,128]{3,1,0,2:T(8,128)(2,1)} %get-tuple-element.389, s32[]{:T(128)} %get-tuple-element.373), kind=kOutput, calls=%fused_computation.8.clone.1 | convolution fusion | flops 543160320 | bytes 9970176 | tf_op jit(solution)/shard_map/while/body/eval_jaxpr/qkgd,nkd->kgqn/dot_general | solution.py:219
  390.8 4.6 fusion.136
  396.7 4.6 fusion.138
  402.9 5.9 %fusion.134 = (f32[2,2,512]{2,1,0:T(2,128)S(1)}, f32[2,1024,512,2]{2,1,3,0:T(8,128)}) fusion(pred[512,1024]{0,1:T(8,128)(4,1)S(1)} %broadcast_compare_fusion.2, bf16[512,2,2,128]{3,0,2,1:T(8,128)(2,1)S(1)} %get-tuple-element.390, bf16[4,1024,2,128]{3,1,0,2:T(8,128)(2,1)} %get-tuple-element.389, s32[]{:T(128)} %get-tuple-element.373), kind=kOutput, calls=%fused_computation.8.clone.1 | convolution fusion | flops 543160320 | bytes 9970176 | tf_op jit(solution)/shard_map/while/body/eval_jaxpr/qkgd,nkd->kgqn/dot_general | solution.py:219
  408.8 4.6 fusion.136
  414.6 4.6 fusion.138
  420.9 5.9 %fusion.134 = (f32[2,2,512]{2,1,0:T(2,128)S(1)}, f32[2,1024,512,2]{2,1,3,0:T(8,128)}) fusion(pred[512,1024]{0,1:T(8,128)(4,1)S(1)} %broadcast_compare_fusion.2, bf16[512,2,2,128]{3,0,2,1:T(8,128)(2,1)S(1)} %get-tuple-element.390, bf16[4,1024,2,128]{3,1,0,2:T(8,128)(2,1)} %get-tuple-element.389, s32[]{:T(128)} %get-tuple-element.373), kind=kOutput, calls=%fused_computation.8.clone.1 | convolution fusion | flops 543160320 | bytes 9970176 | tf_op jit(solution)/shard_map/while/body/eval_jaxpr/qkgd,nkd->kgqn/dot_general | solution.py:219
  426.7 4.6 fusion.136
  432.6 4.6 fusion.138
  438.8 5.9 %fusion.134 = (f32[2,2,512]{2,1,0:T(2,128)S(1)}, f32[2,1024,512,2]{2,1,3,0:T(8,128)}) fusion(pred[512,1024]{0,1:T(8,128)(4,1)S(1)} %broadcast_compare_fusion.2, bf16[512,2,2,128]{3,0,2,1:T(8,128)(2,1)S(1)} %get-tuple-element.390, bf16[4,1024,2,128]{3,1,0,2:T(8,128)(2,1)} %get-tuple-element.389, s32[]{:T(128)} %get-tuple-element.373), kind=kOutput, calls=%fused_computation.8.clone.1 | convolution fusion | flops 543160320 | bytes 9970176 | tf_op jit(solution)/shard_map/while/body/eval_jaxpr/qkgd,nkd->kgqn/dot_general | solution.py:219
  444.7 4.6 fusion.136
  450.5 4.6 fusion.138
  455.6 6.6 %convolution_convert_fusion = bf16[512,4096]{1,0:T(8,128)(2,1)} fusion(bf16[512,512]{0,1:T(8,128)(2,1)S(1)} %bitcast.138, bf16[512,4096]{1,0:T(8,128)(2,1)} %param.37), kind=kOutput, calls=%fused_computation.73 | convolution fusion | flops 2149580800 | bytes 8912896 | tf_op jit(solution)/shard_map/dot_general | solution.py:241
  462.3 43.3 %reduce-scatter.2.cloned.1.call-done = bf16[128,4096]{1,0:T(8,128)(2,1)} async-done(((bf16[512,4096]{1,0:T(8,128)(2,1)}), bf16[128,4096]{1,0:T(8,128)(2,1)}) %reduce-scatter.2.cloned.1.call-update) | async-done | bytes 1048592 | tf_op jit(solution)/shard_map/reduce_scatter | solution.py:240
  (127 shorter events, 39.2 us)
Async XLA Ops:
  6.5 272.9 %copy-start = (bf16[4096,256]{1,0:T(8,128)(2,1)S(1)}, bf16[4096,256]{1,0:T(8,128)(2,1)}, u32[]{:S(2)}) copy-start(bf16[4096,256]{1,0:T(8,128)(2,1)} %param.35) | copy-start | bytes 6291460
  6.5 148.0 %copy-start.7 = (f32[1280]{0:T(1024)S(1)}, f32[1280]{0:T(1024)}, u32[]{:S(2)}) copy-start(f32[1280]{0:T(1024)} %param.25) | copy-start | bytes 15364
  6.5 148.0 %copy-start.6 = (f32[1280]{0:T(1024)S(1)}, f32[1280]{0:T(1024)}, u32[]{:S(2)}) copy-start(f32[1280]{0:T(1024)} %param.26) | copy-start | bytes 15364
  6.5 148.0 %copy-start.5 = (f32[3840]{0:T(1024)S(1)}, f32[3840]{0:T(1024)}, u32[]{:S(2)}) copy-start(f32[3840]{0:T(1024)} %param.28) | copy-start | bytes 46084
  6.5 148.0 %all-gather.6.cloned.1.call-start = ((), (), s32[]{:S(2)}) async-start(), calls=%async_computation.2 | async-start | bytes 11059200 | tf_op jit(solution)/shard_map/all_gather | solution.py:112
  7.3 209.1 %all-gather.8.cloned.1.call-start = ((), (), s32[]{:S(2)}) async-start(), calls=%async_computation.3 | async-start | bytes 3686400 | tf_op jit(solution)/shard_map/all_gather | solution.py:128
  7.3 18.7 %collective-permute-start = (bf16[2,256,1280]{2,1,0:T(8,128)(2,1)}, bf16[2,256,1280]{2,1,0:T(8,128)(2,1)}, u32[]{:S(2)}, u32[]{:S(2)}) collective-permute-start(bf16[2,256,1280]{2,1,0:T(8,128)(2,1)} %param.20), channel_id=1, source_target_pairs={{0,8},{8,0},{16,24},{24,16},{1,9},{9,1},{17,25},{25,17},{2,10},{10... | collective-permute-start | bytes 3932168 | tf_op jit(solution)/shard_map/ppermute | solution.py:18
  170.2 46.2 %copy-start.8 = (f32[1280]{0:T(1024)S(1)}, f32[1280]{0:T(1024)}, u32[]{:S(2)}) copy-start(f32[1280]{0:T(1024)} %param.30) | copy-start | bytes 15364
  222.1 16.9 %copy-start.3 = (f32[4096]{0:T(1024)S(1)}, f32[4096]{0:T(1024)}, u32[]{:S(2)}) copy-start(f32[4096]{0:T(1024)} %param.32) | copy-start | bytes 49156
  226.7 11.3 %all-to-all-start = ((bf16[32,1,2,1280]{3,2,1,0:T(2,128)(2,1)}), bf16[32,1,2,1280]{3,2,1,0:T(2,128)(2,1)S(1)}, u32[]{:S(2)}, u32[]{:S(2)}) async-start(bf16[32,1,2,1280]{3,2,1,0:T(2,128)(2,1)} %broadcast_select_fusion.1), calls=%async_computation | async-start | bytes 327680 | tf_op jit(solution)/shard_map/all_to_all | solution.py:143
  230.0 49.4 %all-gather.10.cloned.1.call-start = ((), (), s32[]{:S(2)}) async-start(), calls=%async_computation.4 | async-start | bytes 5242880 | tf_op jit(solution)/shard_map/all_gather | solution.py:164
  239.0 6.3 %copy-start.4 = (f32[4096]{0:T(1024)S(1)}, f32[4096]{0:T(1024)}, u32[]{:S(2)}) copy-start(f32[4096]{0:T(1024)} %param.33) | copy-start | bytes 49156
  246.6 87.1 %all-gather.12.cloned.1.call-start = ((), (), s32[]{:S(2)}) async-start(), calls=%async_computation.5 | async-start | bytes 2359296 | tf_op jit(solution)/shard_map/all_gather | solution.py:203
  284.4 98.9 %all-gather.14.cloned.1.call-start = ((), (), s32[]{:S(2)}) async-start(), calls=%async_computation.6 | async-start | bytes 2359296 | tf_op jit(solution)/shard_map/all_gather | solution.py:204
  289.5 216.0 %reduce-scatter.2.cloned.1.call-start = ((), (), s32[]{:S(2)}) async-start(), calls=%async_computation.7 | async-start | bytes 5242880 | tf_op jit(solution)/shard_map/reduce_scatter | solution.py:240
  390.8 5.8 %copy-start.2 = (f32[2,1024,512,2]{2,1,3,0:T(8,128)S(1)}, f32[2,1024,512,2]{2,1,3,0:T(8,128)}, u32[]{:S(2)}) copy-start(f32[2,1024,512,2]{2,1,3,0:T(8,128)} %get-tuple-element.359) | copy-start | bytes 25165828 | tf_op jit(solution)/shard_map/while
  408.8 5.8 %copy-start.2 = (f32[2,1024,512,2]{2,1,3,0:T(8,128)S(1)}, f32[2,1024,512,2]{2,1,3,0:T(8,128)}, u32[]{:S(2)}) copy-start(f32[2,1024,512,2]{2,1,3,0:T(8,128)} %get-tuple-element.359) | copy-start | bytes 25165828 | tf_op jit(solution)/shard_map/while
  426.7 5.8 %copy-start.2 = (f32[2,1024,512,2]{2,1,3,0:T(8,128)S(1)}, f32[2,1024,512,2]{2,1,3,0:T(8,128)}, u32[]{:S(2)}) copy-start(f32[2,1024,512,2]{2,1,3,0:T(8,128)} %get-tuple-element.359) | copy-start | bytes 25165828 | tf_op jit(solution)/shard_map/while
  444.7 5.8 %copy-start.2 = (f32[2,1024,512,2]{2,1,3,0:T(8,128)S(1)}, f32[2,1024,512,2]{2,1,3,0:T(8,128)}, u32[]{:S(2)}) copy-start(f32[2,1024,512,2]{2,1,3,0:T(8,128)} %get-tuple-element.359) | copy-start | bytes 25165828 | tf_op jit(solution)/shard_map/while
  455.6 50.0 %copy-start.1 = (bf16[4096,256]{1,0:T(8,128)(2,1)S(1)}, bf16[4096,256]{1,0:T(8,128)(2,1)}, u32[]{:S(2)}) copy-start(bf16[4096,256]{1,0:T(8,128)(2,1)} %param.35) | copy-start | bytes 6291460
Sparse Core Ops, SparseCore 0:
  9.5 144.9 all-gather.5
  156.7 59.6 all-gather.7
  246.7 32.7 all-gather.9
  284.6 49.0 all-gather.11
  335.7 47.5 all-gather.13
  462.4 43.1 reduce-scatter.1
where the time goes:
time: 513 us; the launch traced here: 512 us
  waiting for transfers between devices  341 us (66%)
  matrix products  83.9 us (16%)
  other arithmetic  37.4 us (7%)
  local copies, waits for them, and re-layouts  24.6 us (5%)
  between operations  20.7 us (4%)
    all_gather x1, waiting for transfers between devices, per_device(): lax.all_gather(vit_qkv_w, 'seq', axis=0, tiled=True)  126 us
    all_gather x1, waiting for transfers between devices, per_device(): value_piece = lax.all_gather(values_own, 'seq', axis=0, tiled=True)  49.7 us
    all_gather x1, waiting for transfers between devices, per_device(): lax.all_gather(vit_out_w, 'seq', axis=0, tiled=True)  44.6 us
    reduce_scatter x1, waiting for transfers between devices, per_device(): lax.psum_scatter(jnp.dot(context_tok, wo, preferred_element_type=jnp.floa...  43.3 us
    all_gather x1, waiting for transfers between devices, per_device(): key_piece = lax.all_gather(keys_own, 'seq', axis=0, tiled=True)  37 us
    all_gather x1, waiting for transfers between devices, per_device(): shard_piece = lax.all_gather(normed_tok, 'frame', axis=0, tiled=True)  32 us
    dot_general x4, matrix products, visit(): jnp.einsum('qkgd,nkd->kgqn', grouped_rows, key_block, preferred_element_t...  23.4 us
    reduce_sum x4, other arithmetic, visit(): denominator = denominator * rescale + jnp.sum(expd, axis=-1)  18.6 us
  transfers between devices with their start and end apart: 8, of which 7 were waited for; matrix products, arithmetic and copies ran while one was open for 8% of the time, Pallas kernels for 0%

commit v1 on v0

--- a/solution.py
+++ b/solution.py
@@ -201,7 +201,12 @@
     )
     carry = start_state
     key_piece = lax.all_gather(keys_own, "seq", axis=0, tiled=True)
-    value_piece = lax.all_gather(values_own, "seq", axis=0, tiled=True)
+    ring = [values_own]
+    for hop in range(7):
+        ring.append(lax.ppermute(ring[-1], "seq", [(dev, (dev + 1) % 8) for dev in range(8)]))
+    value_piece = jnp.roll(
+        jnp.concatenate(ring[::-1], axis=0), (lax.axis_index("seq") + 1) * ring[0].shape[0], axis=0
+    )
     piece_rows = key_piece.shape[0]
     inner_rows = math.gcd(piece_rows, 1024)
     steps_n = piece_rows // inner_rows

time: 513 us -> 508 us (level)
  waiting for transfers between devices: 341 us -> 323 us
  local copies, waits for them, and re-layouts: 24.6 us -> 34.6 us
    ppermute x0 -> x7, waiting for transfers between devices: none -> 59.2 us  [per_device(): lax.ppermute(ring[-1], 'seq', [(dev, (dev + 1) % 8) for dev in range(8)])]
    all_gather x1 -> x0, waiting for transfers between devices: 49.7 us -> none  [per_device(): value_piece = lax.all_gather(values_own, 'seq', axis=0, tiled=True)]
    all_gather x1, waiting for transfers between devices: 37 us -> 8.4 us  [per_device(): key_piece = lax.all_gather(keys_own, 'seq', axis=0, tiled=True)]
    unnamed x18 -> x45, local copies, waits for them, and re-layouts: 0.43 us -> 9.6 us
  transfers between devices with their start and end apart: 8 -> 14, of which waited for: 7 -> 13; matrix products, arithmetic and copies ran while one was open for 8% -> 11% of each run, Pallas kernels for 0% -> 0%
where the time goes in v1:
time: 508 us; the launch traced here: 506 us
  waiting for transfers between devices  323 us (64%)
  matrix products  83.9 us (17%)
  other arithmetic  38.2 us (8%)
  local copies, waits for them, and re-layouts  34.6 us (7%)
  between operations  20.5 us (4%)
  starting transfers between devices  5.76 us (1%)
    all_gather x1, waiting for transfers between devices, per_device(): lax.all_gather(vit_qkv_w, 'seq', axis=0, tiled=True)  126 us
    ppermute x7, waiting for transfers between devices, per_device(): lax.ppermute(ring[-1], 'seq', [(dev, (dev + 1) % 8) for dev in range(8)])  59.2 us
    all_gather x1, waiting for transfers between devices, per_device(): lax.all_gather(vit_out_w, 'seq', axis=0, tiled=True)  44.6 us
    reduce_scatter x1, waiting for transfers between devices, per_device(): lax.psum_scatter(jnp.dot(context_tok, wo, preferred_element_type=jnp.floa...  43.3 us
    all_gather x1, waiting for transfers between devices, per_device(): shard_piece = lax.all_gather(normed_tok, 'frame', axis=0, tiled=True)  32.8 us
    dot_general x4, matrix products, visit(): jnp.einsum('qkgd,nkd->kgqn', grouped_rows, key_block, preferred_element_t...  23.4 us
    reduce_sum x4, other arithmetic, visit(): denominator = denominator * rescale + jnp.sum(expd, axis=-1)  18.6 us
    dot_general x4, matrix products, visit(): jnp.einsum('kgqn,nkd->kgqd', expd.astype(jnp.bfloat16), value_block, pref...  18.3 us
  transfers between devices with their start and end apart: 14, of which 13 were waited for; matrix products, arithmetic and copies ran while one was open for 11% of the time, Pallas kernels for 0%

profile of v1, /device:TPU:0, one launch (start us, length us, event | category | flops | bytes accessed | tf_op | source)
XLA Modules:
  0.0 506.3 jit_solution(15250584760435057879)
XLA Ops:
  28.3 126.2 %all-gather.5.cloned.1.call-done = bf16[1280,3840]{1,0:T(8,128)(2,1)} async-done(((bf16[160,3840]{1,0:T(8,128)(2,1)}), bf16[1280,3840]{1,0:T(8,128)(2,1)}) %all-gather.5.cloned.1.call-update) | async-done | bytes 9830416 | tf_op jit(solution)/shard_map/all_gather | solution.py:112
  154.5 7.9 %fusion.48 = bf16[256,3840]{1,0:T(8,128)(2,1)} fusion(bf16[1280,3840]{1,0:T(8,128)(2,1)} %all-gather.5.cloned.1.call-done, f32[3840]{0:T(1024)S(1)} %copy-done.11, bf16[1,256,1280]{2,1,0:T(8,128)(2,1)S(1)} %get-tuple-element.277, f32[1280]{0:T(1024)S(1)} %copy-done.12, f32[1280]{0:T(1024)S(1)} %copy-done.13, f32[256]{0:T(256)S(1)} %add_rsqrt_fusion, ...), kind=kOutput, calls=%fused_computation.75 | convolution fusion | flops 2520514560 | bytes 12479488 | tf_op jit(solution)/shard_map/dot_general | solution.py:43
  171.7 44.6 %all-gather.7.cloned.1.call-done = bf16[1280,1280]{1,0:T(8,128)(2,1)} async-done(((bf16[160,1280]{1,0:T(8,128)(2,1)}), bf16[1280,1280]{1,0:T(8,128)(2,1)}) %all-gather.7.cloned.1.call-update) | async-done | bytes 3276816 | tf_op jit(solution)/shard_map/all_gather | solution.py:128
  216.3 4.1 fusion.55
  230.3 7.7 %all-to-all-done = bf16[32,1,2,1280]{3,2,1,0:T(2,128)(2,1)S(1)} async-done(((bf16[32,1,2,1280]{3,2,1,0:T(2,128)(2,1)}), bf16[32,1,2,1280]{3,2,1,0:T(2,128)(2,1)S(1)}, u32[]{:S(2)}, u32[]{:S(2)}) %all-to-all-start) | async-done | bytes 163872 | tf_op jit(solution)/shard_map/all_to_all | solution.py:143
  239.0 6.3 %multiply_reduce_fusion = (f32[128]{0:T(128)S(1)}, f32[128,4096]{1,0:T(8,128)S(1)}) fusion(bf16[128,1,4096]{2,0,1:T(8,128)(2,1)} %param.24, f32[4096]{0:T(1024)S(1)} %copy-done.9, bf16[128,1280]{1,0:T(8,128)(2,1)S(1)} %gather_fusion.4, bf16[1280,4096]{1,0:T(8,128)(2,1)} %param.31, pred[128]{0:T(512)(128)(4,1)S(1)} %compare_and_fusion.1), kind=kOutput, calls=%fused_computation.93 | convolution fusion | flops 1345322880 | bytes 13976192 | tf_op jit(solution)/shard_map/dot_general | solution.py:153
  246.6 32.8 %all-gather.9.cloned.1.call-done = bf16[512,4096]{1,0:T(8,128)(2,1)} async-done(((bf16[128,4096]{1,0:T(8,128)(2,1)}), bf16[512,4096]{1,0:T(8,128)(2,1)}) %all-gather.9.cloned.1.call-update) | async-done | bytes 4194320 | tf_op jit(solution)/shard_map/all_gather | solution.py:164
  284.7 9.7 %collective-permute-done.1 = bf16[512,2,128]{2,0,1:T(8,128)(2,1)S(1)} collective-permute-done((bf16[512,2,128]{2,0,1:T(8,128)(2,1)S(1)}, bf16[512,2,128]{2,0,1:T(8,128)(2,1)S(1)}, u32[]{:S(2)}, u32[]{:S(2)}) %collective-permute-start.1) | collective-permute-done | bytes 262176 | tf_op jit(solution)/shard_map/ppermute | solution.py:206
  295.2 9.5 %collective-permute-done.2 = bf16[512,2,128]{2,0,1:T(8,128)(2,1)S(1)} collective-permute-done((bf16[512,2,128]{2,0,1:T(8,128)(2,1)S(1)}, bf16[512,2,128]{2,0,1:T(8,128)(2,1)S(1)}, u32[]{:S(2)}, u32[]{:S(2)}) %collective-permute-start.2) | collective-permute-done | bytes 262176 | tf_op jit(solution)/shard_map/ppermute | solution.py:206
  304.6 4.2 fusion.103
  309.3 4.7 collective-permute-done.3
  314.2 8.9 %collective-permute-done.4 = bf16[512,2,128]{2,0,1:T(8,128)(2,1)S(1)} collective-permute-done((bf16[512,2,128]{2,0,1:T(8,128)(2,1)S(1)}, bf16[512,2,128]{2,0,1:T(8,128)(2,1)S(1)}, u32[]{:S(2)}, u32[]{:S(2)}) %collective-permute-start.4) | collective-permute-done | bytes 262176 | tf_op jit(solution)/shard_map/ppermute | solution.py:206
  324.1 8.2 %collective-permute-done.5 = bf16[512,2,128]{2,0,1:T(8,128)(2,1)} collective-permute-done((bf16[512,2,128]{2,0,1:T(8,128)(2,1)S(1)}, bf16[512,2,128]{2,0,1:T(8,128)(2,1)}, u32[]{:S(2)}, u32[]{:S(2)}) %collective-permute-start.5) | collective-permute-done | bytes 262176 | tf_op jit(solution)/shard_map/ppermute | solution.py:206
  332.3 5.9 %fusion.104 = f32[512,512]{0,1:T(8,128)S(1)} fusion(bf16[512,4096]{1,0:T(8,128)(2,1)} %all-gather.9.cloned.1.call-done, bf16[4096,512]{1,0:T(8,128)(2,1)} %param.34), kind=kOutput, calls=%fused_computation.230 | convolution fusion | flops 2147483648 | bytes 9437184 | tf_op jit(solution)/shard_map/dot_general | solution.py:167
  338.3 10.6 %collective-permute-done.6 = bf16[512,2,128]{2,0,1:T(8,128)(2,1)} collective-permute-done((bf16[512,2,128]{2,0,1:T(8,128)(2,1)}, bf16[512,2,128]{2,0,1:T(8,128)(2,1)}, u32[]{:S(2)}, u32[]{:S(2)}) %collective-permute-start.6) | collective-permute-done | bytes 262176 | tf_op jit(solution)/shard_map/ppermute | solution.py:206
  350.7 7.6 %collective-permute-done.7 = bf16[512,2,128]{2,0,1:T(8,128)(2,1)} collective-permute-done((bf16[512,2,128]{2,0,1:T(8,128)(2,1)}, bf16[512,2,128]{2,0,1:T(8,128)(2,1)}, u32[]{:S(2)}, u32[]{:S(2)}) %collective-permute-start.7) | collective-permute-done | bytes 262176 | tf_op jit(solution)/shard_map/ppermute | solution.py:206
  369.1 8.4 %all-gather.11.cloned.1.call-done = bf16[4096,2,128]{2,0,1:T(8,128)(2,1)} async-done(((bf16[512,2,128]{2,0,1:T(8,128)(2,1)}), bf16[4096,2,128]{2,0,1:T(8,128)(2,1)}) %all-gather.11.cloned.1.call-update) | async-done | bytes 2097168 | tf_op jit(solution)/shard_map/all_gather | solution.py:203
  377.5 71.8 %while.20 = (s32[]{:T(128)}, f32[2,2,512]{2,1,0:T(2,128)S(1)}, f32[2,2,512]{2,1,0:T(2,128)S(1)}, f32[2,2,512,128]{3,2,1,0:T(8,128)S(1)}, s32[4]{0:T(128)S(1)}, /...) while((s32[]{:T(128)}, f32[2,2,512]{2,1,0:T(2,128)S(1)}, ...), condition=%wide.region_12.13_spmd.clone, body=%wide.region_9.12_spmd.clone.sunk | while | flops 1102377984 | bytes 64631976 | solution.py:241
  379.2 5.9 %fusion.134 = (f32[2,2,512]{2,1,0:T(2,128)S(1)}, f32[2,1024,512,2]{2,1,3,0:T(8,128)}) fusion(pred[512,1024]{0,1:T(8,128)(4,1)S(1)} %broadcast_compare_fusion.2, bf16[512,2,2,128]{3,0,2,1:T(8,128)(2,1)S(1)} %get-tuple-element.390, bf16[4,1024,2,128]{3,1,0,2:T(8,128)(2,1)} %get-tuple-element.389, s32[]{:T(128)} %get-tuple-element.373), kind=kOutput, calls=%fused_computation.8.clone.1 | convolution fusion | flops 543160320 | bytes 9970176 | tf_op jit(solution)/shard_map/while/body/eval_jaxpr/qkgd,nkd->kgqn/dot_general | solution.py:224
  385.0 4.6 fusion.136
  390.9 4.6 fusion.138
  397.1 5.9 %fusion.134 = (f32[2,2,512]{2,1,0:T(2,128)S(1)}, f32[2,1024,512,2]{2,1,3,0:T(8,128)}) fusion(pred[512,1024]{0,1:T(8,128)(4,1)S(1)} %broadcast_compare_fusion.2, bf16[512,2,2,128]{3,0,2,1:T(8,128)(2,1)S(1)} %get-tuple-element.390, bf16[4,1024,2,128]{3,1,0,2:T(8,128)(2,1)} %get-tuple-element.389, s32[]{:T(128)} %get-tuple-element.373), kind=kOutput, calls=%fused_computation.8.clone.1 | convolution fusion | flops 543160320 | bytes 9970176 | tf_op jit(solution)/shard_map/while/body/eval_jaxpr/qkgd,nkd->kgqn/dot_general | solution.py:224
  403.0 4.6 fusion.136
  408.8 4.6 fusion.138
  415.1 5.9 %fusion.134 = (f32[2,2,512]{2,1,0:T(2,128)S(1)}, f32[2,1024,512,2]{2,1,3,0:T(8,128)}) fusion(pred[512,1024]{0,1:T(8,128)(4,1)S(1)} %broadcast_compare_fusion.2, bf16[512,2,2,128]{3,0,2,1:T(8,128)(2,1)S(1)} %get-tuple-element.390, bf16[4,1024,2,128]{3,1,0,2:T(8,128)(2,1)} %get-tuple-element.389, s32[]{:T(128)} %get-tuple-element.373), kind=kOutput, calls=%fused_computation.8.clone.1 | convolution fusion | flops 543160320 | bytes 9970176 | tf_op jit(solution)/shard_map/while/body/eval_jaxpr/qkgd,nkd->kgqn/dot_general | solution.py:224
  421.0 4.6 fusion.136
  426.8 4.6 fusion.138
  433.0 5.9 %fusion.134 = (f32[2,2,512]{2,1,0:T(2,128)S(1)}, f32[2,1024,512,2]{2,1,3,0:T(8,128)}) fusion(pred[512,1024]{0,1:T(8,128)(4,1)S(1)} %broadcast_compare_fusion.2, bf16[512,2,2,128]{3,0,2,1:T(8,128)(2,1)S(1)} %get-tuple-element.390, bf16[4,1024,2,128]{3,1,0,2:T(8,128)(2,1)} %get-tuple-element.389, s32[]{:T(128)} %get-tuple-element.373), kind=kOutput, calls=%fused_computation.8.clone.1 | convolution fusion | flops 543160320 | bytes 9970176 | tf_op jit(solution)/shard_map/while/body/eval_jaxpr/qkgd,nkd->kgqn/dot_general | solution.py:224
  438.9 4.6 fusion.136
  444.7 4.6 fusion.138
  449.8 6.7 %convolution_convert_fusion = bf16[512,4096]{1,0:T(8,128)(2,1)} fusion(bf16[512,512]{0,1:T(8,128)(2,1)S(1)} %bitcast.138, bf16[512,4096]{1,0:T(8,128)(2,1)} %param.37), kind=kOutput, calls=%fused_computation.73 | convolution fusion | flops 2149580800 | bytes 8912896 | tf_op jit(solution)/shard_map/dot_general | solution.py:246
  456.5 43.3 %reduce-scatter.2.cloned.1.call-done = bf16[128,4096]{1,0:T(8,128)(2,1)} async-done(((bf16[512,4096]{1,0:T(8,128)(2,1)}), bf16[128,4096]{1,0:T(8,128)(2,1)}) %reduce-scatter.2.cloned.1.call-update) | async-done | bytes 1048592 | tf_op jit(solution)/shard_map/reduce_scatter | solution.py:245
  (167 shorter events, 68.0 us)
Async XLA Ops:
  6.5 272.9 %copy-start = (bf16[4096,256]{1,0:T(8,128)(2,1)S(1)}, bf16[4096,256]{1,0:T(8,128)(2,1)}, u32[]{:S(2)}) copy-start(bf16[4096,256]{1,0:T(8,128)(2,1)} %param.36) | copy-start | bytes 6291460
  6.5 147.9 %copy-start.13 = (f32[1280]{0:T(1024)S(1)}, f32[1280]{0:T(1024)}, u32[]{:S(2)}) copy-start(f32[1280]{0:T(1024)} %param.25) | copy-start | bytes 15364
  6.5 147.9 %copy-start.12 = (f32[1280]{0:T(1024)S(1)}, f32[1280]{0:T(1024)}, u32[]{:S(2)}) copy-start(f32[1280]{0:T(1024)} %param.26) | copy-start | bytes 15364
  6.5 148.0 %copy-start.11 = (f32[3840]{0:T(1024)S(1)}, f32[3840]{0:T(1024)}, u32[]{:S(2)}) copy-start(f32[3840]{0:T(1024)} %param.28) | copy-start | bytes 46084
  6.5 147.9 %all-gather.5.cloned.1.call-start = ((), (), s32[]{:S(2)}) async-start(), calls=%async_computation.2 | async-start | bytes 11059200 | tf_op jit(solution)/shard_map/all_gather | solution.py:112
  7.3 209.1 %all-gather.7.cloned.1.call-start = ((), (), s32[]{:S(2)}) async-start(), calls=%async_computation.3 | async-start | bytes 3686400 | tf_op jit(solution)/shard_map/all_gather | solution.py:128
  7.3 18.8 %collective-permute-start = (bf16[2,256,1280]{2,1,0:T(8,128)(2,1)}, bf16[2,256,1280]{2,1,0:T(8,128)(2,1)}, u32[]{:S(2)}, u32[]{:S(2)}) collective-permute-start(bf16[2,256,1280]{2,1,0:T(8,128)(2,1)} %param.20), channel_id=1, source_target_pairs={{0,8},{8,0},{16,24},{24,16},{1,9},{9,1},{17,25},{25,17},{2,10},{10... | collective-permute-start | bytes 3932168 | tf_op jit(solution)/shard_map/ppermute | solution.py:18
  170.1 46.2 %copy-start.14 = (f32[1280]{0:T(1024)S(1)}, f32[1280]{0:T(1024)}, u32[]{:S(2)}) copy-start(f32[1280]{0:T(1024)} %param.30) | copy-start | bytes 15364
  222.1 16.9 %copy-start.9 = (f32[4096]{0:T(1024)S(1)}, f32[4096]{0:T(1024)}, u32[]{:S(2)}) copy-start(f32[4096]{0:T(1024)} %param.32) | copy-start | bytes 49156
  226.7 11.3 %all-to-all-start = ((bf16[32,1,2,1280]{3,2,1,0:T(2,128)(2,1)}), bf16[32,1,2,1280]{3,2,1,0:T(2,128)(2,1)S(1)}, u32[]{:S(2)}, u32[]{:S(2)}) async-start(bf16[32,1,2,1280]{3,2,1,0:T(2,128)(2,1)} %broadcast_select_fusion.1), calls=%async_computation | async-start | bytes 327680 | tf_op jit(solution)/shard_map/all_to_all | solution.py:143
  230.0 49.4 %all-gather.9.cloned.1.call-start = ((), (), s32[]{:S(2)}) async-start(), calls=%async_computation.4 | async-start | bytes 5242880 | tf_op jit(solution)/shard_map/all_gather | solution.py:164
  239.0 6.3 %copy-start.10 = (f32[4096]{0:T(1024)S(1)}, f32[4096]{0:T(1024)}, u32[]{:S(2)}) copy-start(f32[4096]{0:T(1024)} %param.33) | copy-start | bytes 49156
  246.6 130.9 %all-gather.11.cloned.1.call-start = ((), (), s32[]{:S(2)}) async-start(), calls=%async_computation.5 | async-start | bytes 2359296 | tf_op jit(solution)/shard_map/all_gather | solution.py:203
  283.1 11.2 %collective-permute-start.1 = (bf16[512,2,128]{2,0,1:T(8,128)(2,1)S(1)}, bf16[512,2,128]{2,0,1:T(8,128)(2,1)S(1)}, u32[]{:S(2)}, u32[]{:S(2)}) collective-permute-start(bf16[512,2,128]{2,0,1:T(8,128)(2,1)S(1)} %copy.91), channel_id=1, source_target_pairs={{0,1},{1,2},{2,3},{3,4},{4,5},{5,6},{6,7},{7,0},{8,9},{9,10},{10,1... | collective-permute-start | bytes 786440 | tf_op jit(solution)/shard_map/ppermute | solution.py:206
  294.3 10.3 %collective-permute-start.2 = (bf16[512,2,128]{2,0,1:T(8,128)(2,1)S(1)}, bf16[512,2,128]{2,0,1:T(8,128)(2,1)S(1)}, u32[]{:S(2)}, u32[]{:S(2)}) collective-permute-start(bf16[512,2,128]{2,0,1:T(8,128)(2,1)S(1)} %collective-permute-done.1), channel_id=1, source_target_pairs={{0,1},{1,2},{2,3},{3,4},{4,5},{5,6},{6,7},{7,0},{8,9},{9,10},{10,1... | collective-permute-start | bytes 786440 | tf_op jit(solution)/shard_map/ppermute | solution.py:206
  304.6 4.3 copy-start.3
  304.6 9.4 %collective-permute-start.3 = (bf16[512,2,128]{2,0,1:T(8,128)(2,1)S(1)}, bf16[512,2,128]{2,0,1:T(8,128)(2,1)S(1)}, u32[]{:S(2)}, u32[]{:S(2)}) collective-permute-start(bf16[512,2,128]{2,0,1:T(8,128)(2,1)S(1)} %collective-permute-done.2), channel_id=1, source_target_pairs={{0,1},{1,2},{2,3},{3,4},{4,5},{5,6},{6,7},{7,0},{8,9},{9,10},{10,1... | collective-permute-start | bytes 786440 | tf_op jit(solution)/shard_map/ppermute | solution.py:206
  314.1 24.2 %copy-start.5 = (bf16[512,2,128]{2,0,1:T(8,128)(2,1)}, bf16[512,2,128]{2,0,1:T(8,128)(2,1)S(1)}, u32[]{:S(2)}) copy-start(bf16[512,2,128]{2,0,1:T(8,128)(2,1)S(1)} %collective-permute-done.3) | copy-start | bytes 786436
  314.1 9.1 %collective-permute-start.4 = (bf16[512,2,128]{2,0,1:T(8,128)(2,1)S(1)}, bf16[512,2,128]{2,0,1:T(8,128)(2,1)S(1)}, u32[]{:S(2)}, u32[]{:S(2)}) collective-permute-start(bf16[512,2,128]{2,0,1:T(8,128)(2,1)S(1)} %collective-permute-done.3), channel_id=1, source_target_pairs={{0,1},{1,2},{2,3},{3,4},{4,5},{5,6},{6,7},{7,0},{8,9},{9,10},{10,1... | collective-permute-start | bytes 786440 | tf_op jit(solution)/shard_map/ppermute | solution.py:206
  323.1 15.1 %copy-start.7 = (bf16[512,2,128]{2,0,1:T(8,128)(2,1)}, bf16[512,2,128]{2,0,1:T(8,128)(2,1)S(1)}, u32[]{:S(2)}) copy-start(bf16[512,2,128]{2,0,1:T(8,128)(2,1)S(1)} %collective-permute-done.4) | copy-start | bytes 786436
  323.1 9.2 %collective-permute-start.5 = (bf16[512,2,128]{2,0,1:T(8,128)(2,1)S(1)}, bf16[512,2,128]{2,0,1:T(8,128)(2,1)}, u32[]{:S(2)}, u32[]{:S(2)}) collective-permute-start(bf16[512,2,128]{2,0,1:T(8,128)(2,1)S(1)} %collective-permute-done.4), channel_id=1, source_target_pairs={{0,1},{1,2},{2,3},{3,4},{4,5},{5,6},{6,7},{7,0},{8,9},{9,10},{10,1... | collective-permute-start | bytes 786440 | tf_op jit(solution)/shard_map/ppermute | solution.py:206
  324.0 175.8 %reduce-scatter.2.cloned.1.call-start = ((), (), s32[]{:S(2)}) async-start(), calls=%async_computation.6 | async-start | bytes 5242880 | tf_op jit(solution)/shard_map/reduce_scatter | solution.py:245
  332.3 16.6 %collective-permute-start.6 = (bf16[512,2,128]{2,0,1:T(8,128)(2,1)}, bf16[512,2,128]{2,0,1:T(8,128)(2,1)}, u32[]{:S(2)}, u32[]{:S(2)}) collective-permute-start(bf16[512,2,128]{2,0,1:T(8,128)(2,1)} %collective-permute-done.5), channel_id=1, source_target_pairs={{0,1},{1,2},{2,3},{3,4},{4,5},{5,6},{6,7},{7,0},{8,9},{9,10},{10,1... | collective-permute-start | bytes 786440 | tf_op jit(solution)/shard_map/ppermute | solution.py:206
  348.9 9.5 %collective-permute-start.7 = (bf16[512,2,128]{2,0,1:T(8,128)(2,1)}, bf16[512,2,128]{2,0,1:T(8,128)(2,1)}, u32[]{:S(2)}, u32[]{:S(2)}) collective-permute-start(bf16[512,2,128]{2,0,1:T(8,128)(2,1)} %collective-permute-done.6), channel_id=1, source_target_pairs={{0,1},{1,2},{2,3},{3,4},{4,5},{5,6},{6,7},{7,0},{8,9},{9,10},{10,1... | collective-permute-start | bytes 786440 | tf_op jit(solution)/shard_map/ppermute | solution.py:206
  349.3 13.0 %copy-start.6 = (bf16[512,2,128]{2,0,1:T(8,128)(2,1)S(1)}, bf16[512,2,128]{2,0,1:T(8,128)(2,1)}, u32[]{:S(2)}) copy-start(bf16[512,2,128]{2,0,1:T(8,128)(2,1)} %copy-done.5) | copy-start | bytes 786436
  349.6 17.9 %copy-start.4 = (bf16[512,2,128]{2,0,1:T(8,128)(2,1)S(1)}, bf16[512,2,128]{2,0,1:T(8,128)(2,1)}, u32[]{:S(2)}) copy-start(bf16[512,2,128]{2,0,1:T(8,128)(2,1)} %copy-done.3) | copy-start | bytes 786436
  363.4 14.1 %copy-start.8 = (bf16[512,2,2,128]{3,0,2,1:T(8,128)(2,1)S(1)}, bf16[512,2,2,128]{3,0,2,1:T(8,128)(2,1)}, u32[]{:S(2)}) copy-start(bf16[512,2,2,128]{3,0,2,1:T(8,128)(2,1)} %pad_maximum_fusion) | copy-start | bytes 1572868
  385.0 5.8 %copy-start.2 = (f32[2,1024,512,2]{2,1,3,0:T(8,128)S(1)}, f32[2,1024,512,2]{2,1,3,0:T(8,128)}, u32[]{:S(2)}) copy-start(f32[2,1024,512,2]{2,1,3,0:T(8,128)} %get-tuple-element.359) | copy-start | bytes 25165828 | tf_op jit(solution)/shard_map/while
  403.0 5.8 %copy-start.2 = (f32[2,1024,512,2]{2,1,3,0:T(8,128)S(1)}, f32[2,1024,512,2]{2,1,3,0:T(8,128)}, u32[]{:S(2)}) copy-start(f32[2,1024,512,2]{2,1,3,0:T(8,128)} %get-tuple-element.359) | copy-start | bytes 25165828 | tf_op jit(solution)/shard_map/while
  420.9 5.8 %copy-start.2 = (f32[2,1024,512,2]{2,1,3,0:T(8,128)S(1)}, f32[2,1024,512,2]{2,1,3,0:T(8,128)}, u32[]{:S(2)}) copy-start(f32[2,1024,512,2]{2,1,3,0:T(8,128)} %get-tuple-element.359) | copy-start | bytes 25165828 | tf_op jit(solution)/shard_map/while
  438.9 5.8 %copy-start.2 = (f32[2,1024,512,2]{2,1,3,0:T(8,128)S(1)}, f32[2,1024,512,2]{2,1,3,0:T(8,128)}, u32[]{:S(2)}) copy-start(f32[2,1024,512,2]{2,1,3,0:T(8,128)} %get-tuple-element.359) | copy-start | bytes 25165828 | tf_op jit(solution)/shard_map/while
  449.8 50.0 %copy-start.1 = (bf16[4096,256]{1,0:T(8,128)(2,1)S(1)}, bf16[4096,256]{1,0:T(8,128)(2,1)}, u32[]{:S(2)}) copy-start(bf16[4096,256]{1,0:T(8,128)(2,1)} %param.36) | copy-start | bytes 6291460
Sparse Core Ops, SparseCore 0:
  9.5 144.9 all-gather.4
  156.7 59.6 all-gather.6
  246.7 32.7 all-gather.8
  324.1 53.3 all-gather.10
  456.6 43.1 reduce-scatter.1
